TPU v7x, 32 devices: a whole 2x2x4 slice. The times are simulated.
32 devices in a mesh: replica: 8 (over z, core), tp: 4 (over y, x).
Axes of the slice: x: 2, y: 2, z: 4, core: 2. Of those that a mesh axis runs over, the one named last changes fastest.
Arguments:
- token_ids: int32 [128], replicated, may hold values from 0 to 8191
- embed_table: bfloat16 [8192, 8192], P('replica', 'tp'), may hold values from -6 to 6
- norm_gain: bfloat16 [8192], replicated, may hold values from 0.099609375 to 1.8984375
- w_query: bfloat16 [8192, 4096], P(('replica', 'tp')), may hold values from -0.0625 to 0.0625
- w_keyvalue: bfloat16 [8192, 2, 512], P(('replica', 'tp')), may hold values from -0.0625 to 0.0625
- key_cache: bfloat16 [512, 1024, 128], P(('replica', 'tp')), may hold values from -360 to 360
- value_cache: bfloat16 [512, 1024, 128], P(('replica', 'tp')), may hold values from -6 to 6
- cache_lengths: int32 [128], P('replica'), may hold values from 1 to 1024, as said below
Outputs:
- context: bfloat16 [512, 1024], P(('replica', 'tp'))
- query_weight_tp: bfloat16 [8192, 4096], P(None, 'tp')
- keyvalue_weight_tp: bfloat16 [8192, 2, 512], P(None, None, 'tp')
Inputs may be any that keep to these rules, and one draw needn't show every extreme that they name: `cache_lengths`: some sequence has exactly 1024 filled slots.
All inputs are finite; a program needn't handle non-finite values.
Results may differ from a plain program's by a relative error of at most 0.019.
The roundings to bfloat16 on the way count: a program that leaves them out, or rounds other values in their place, can miss the bound.
Values may be sent and summed in bfloat16 or wider, within the bound.
A program may use at most 128 MiB of HBM per device.

v0:
```python
import jax
import jax.numpy as jnp
from jax import lax
from jax.sharding import PartitionSpec as P


def attend(query, keys, values, key_new, value_new, lengths):
    scale = query.shape[-1] ** (-0.5)
    scores = jnp.einsum("rgd,rcd->rgc", query, keys, preferred_element_type=jnp.float32) * scale
    position = lax.broadcasted_iota(jnp.int32, scores.shape, 2)
    scores = jnp.where(position < lengths[:, None, None], scores, -jnp.inf)
    own = jnp.einsum("rgd,rd->rg", query, key_new, preferred_element_type=jnp.float32) * scale
    top = jnp.maximum(jnp.max(scores, axis=2), own)
    weights = jnp.exp(scores - top[:, :, None])
    own_weight = jnp.exp(own - top)
    total = jnp.sum(weights, axis=2) + own_weight
    weights = (weights / total[:, :, None]).astype(jnp.bfloat16)
    own_weight = (own_weight / total).astype(jnp.bfloat16)
    context = jnp.einsum("rgc,rcd->rgd", weights, values, preferred_element_type=jnp.float32)
    context = (
        context
        + own_weight.astype(jnp.float32)[:, :, None] * value_new.astype(jnp.float32)[:, None, :]
    )
    return context.astype(jnp.bfloat16)


def per_device(
    token_ids, embed_table, norm_gain, w_query, w_keyvalue, key_cache, value_cache, cache_lengths
):
    group_index = lax.axis_index("replica")
    tp_index = lax.axis_index("tp")
    vocab_rows, feature_cols = embed_table.shape
    batch = cache_lengths.shape[0]
    first_id = group_index * vocab_rows
    picked = token_ids - first_id
    columns = lax.broadcasted_iota(jnp.int32, (batch * lax.axis_size("replica"), vocab_rows), 1)
    onehot = (picked[:, None] == columns).astype(jnp.bfloat16)
    embedded = lax.psum_scatter(
        jnp.dot(onehot, embed_table, preferred_element_type=jnp.float32),
        "replica",
        scatter_dimension=0,
        tiled=True,
    ).astype(jnp.bfloat16)
    whole = lax.all_gather(embedded, "tp", axis=1, tiled=True)
    values32 = whole.astype(jnp.float32)
    mean_square = jnp.mean(values32 * values32, axis=1, keepdims=True)
    normed = (values32 * lax.rsqrt(mean_square + 1e-05) * norm_gain.astype(jnp.float32)).astype(
        jnp.bfloat16
    )
    width = normed.shape[1]
    query_rows = w_query.reshape(w_query.shape[0], 1, w_query.shape[1])
    query_mid, pair_mid = (
        lax.all_to_all(query_rows, "tp", split_axis=2, concat_axis=0, tiled=True),
        lax.all_to_all(w_keyvalue, "tp", split_axis=2, concat_axis=0, tiled=True),
    )
    flat_query = query_mid.reshape(query_mid.shape[0], query_mid.shape[2])
    pair_cols = pair_mid.shape[2]
    flat_pair = pair_mid.reshape(pair_mid.shape[0], 2 * pair_cols)
    query_full, pair_full = (
        lax.all_gather(flat_query, "replica", axis=0, tiled=True),
        lax.all_gather(flat_pair, "replica", axis=0, tiled=True),
    )
    query_acc = jnp.dot(normed, query_full, preferred_element_type=jnp.float32)
    pair_acc = jnp.dot(normed, pair_full, preferred_element_type=jnp.float32)
    query_local = query_acc.astype(jnp.bfloat16)
    pair_local = pair_acc.astype(jnp.bfloat16).reshape(batch, 2, pair_cols)
    query_heads, pair_heads = (
        lax.all_gather(query_local, "tp", axis=1, tiled=True),
        lax.all_gather(pair_local, "tp", axis=2, tiled=True),
    )
    head_size = key_cache.shape[2]
    kv_heads = pair_heads.shape[2] // head_size
    group = query_heads.shape[1] // (kv_heads * head_size)
    rows_here = key_cache.shape[0]
    first_row = tp_index * rows_here
    query_grouped = (
        query_heads.reshape(batch, kv_heads, group, head_size)
        .transpose(1, 0, 2, 3)
        .reshape(kv_heads * batch, group, head_size)
    )
    key_grouped = (
        pair_heads[:, 0]
        .reshape(batch, kv_heads, head_size)
        .transpose(1, 0, 2)
        .reshape(kv_heads * batch, head_size)
    )
    value_grouped = (
        pair_heads[:, 1]
        .reshape(batch, kv_heads, head_size)
        .transpose(1, 0, 2)
        .reshape(kv_heads * batch, head_size)
    )
    query_mine = lax.dynamic_slice_in_dim(query_grouped, first_row, rows_here, 0)
    key_mine = lax.dynamic_slice_in_dim(key_grouped, first_row, rows_here, 0)
    value_mine = lax.dynamic_slice_in_dim(value_grouped, first_row, rows_here, 0)
    sequence = (first_row + lax.broadcasted_iota(jnp.int32, (rows_here,), 0)) % batch
    matches = sequence[:, None] == lax.broadcasted_iota(jnp.int32, (rows_here, batch), 1)
    row_lengths = jnp.sum(jnp.where(matches, cache_lengths[None, :], 0), axis=1)
    context = attend(query_mine, key_cache, value_cache, key_mine, value_mine, row_lengths)
    context = context.reshape(rows_here, group * head_size)
    return (context, query_full, pair_full.reshape(width, 2, pair_cols))


def solution(mesh):
    return jax.shard_map(
        per_device,
        mesh=mesh,
        in_specs=(
            P(),
            P("replica", "tp"),
            P(),
            P(("replica", "tp"), None),
            P(("replica", "tp"), None, None),
            P(("replica", "tp"), None, None),
            P(("replica", "tp"), None, None),
            P("replica"),
        ),
        out_specs=(P(("replica", "tp"), None), P(None, "tp"), P(None, None, "tp")),
        check_vma=False,
    )
```

profile of v0, /device:TPU:0, one launch (start us, length us, event | category | flops | bytes accessed | tf_op | source)
XLA Modules:
  0.0 279.0 jit_solution(18418797829905342189)
XLA Ops:
  7.2 0.0 copy-start.3
  7.2 0.0 reduce-scatter.2.cloned.1.call-start
  7.2 0.7 broadcast_subtract_fusion
  7.9 3.9 %fusion.6 = f32[128,2048]{1,0:T(8,128)} fusion(bf16[1024,2048]{1,0:T(8,128)(2,1)} %param.9, s32[128]{0:T(128)S(1)} %broadcast_subtract_fusion), kind=kOutput, calls=%fused_computation.17 | convolution fusion | flops 537001984 | bytes 5243392 | tf_op jit(solution)/shard_map/dot_general | solution.py:39
  11.8 0.0 copy-start.2
  11.9 0.0 reduce-scatter.2.cloned.1.call-update
  11.9 0.0 all-gather.5.cloned.1.call-start
  11.9 0.0 copy-done.3
  11.9 1.0 copy.59
  12.9 13.5 %all_to_all.30 = bf16[256,2,512]{0,1,2:T(2,128)(2,1)S(1)} all-to-all(bf16[256,2,512]{0,1,2:T(2,128)(2,1)S(1)} %copy.59), channel_id=1, replica_groups=mesh['replica'=8,'tp'=4] {'tp'}, dimensions={2} | all-to-all | bytes 1048576 | tf_op jit(solution)/shard_map/all_to_all | solution.py:54
  26.5 0.6 copy.60
  27.1 0.9 copy.76
  28.0 0.0 all-gather.5.cloned.1.call-update
  28.0 0.0 all-gather.3.cloned.1.call-start
  28.1 0.0 copy-done.2
  28.1 7.1 %copy.56 = bf16[256,1,4096]{0,1,2:T(2,128)(2,1)} copy(bf16[256,1,4096]{2,0,1:T(8,128)(2,1)S(1)} %bitcast.52) | data formatting | bytes 4194304 | tf_op jit(solution)/shard_map/reshape | solution.py:51
  35.1 0.5 broadcast.60
  35.6 21.6 %reduce = bf16[4096,256]{1,0:T(8,128)(2,1)S(1)} reduce(bf16[4096,1,256]{2,1,0:T(2,128)(2,1)} %bitcast.48, bf16[]{:T(256)} %broadcast.60), dimensions={1}, to_apply=%bitcast.36.reduce_sub_computation | reduce | bytes 4194306
  57.2 2.1 reshape.81
  59.3 27.9 %all_to_all.31 = bf16[4,2,131072]{2,1,0:T(2,128)(2,1)S(1)} all-to-all(bf16[4,2,131072]{2,1,0:T(2,128)(2,1)} %reshape.81), channel_id=1, replica_groups=mesh['replica'=8,'tp'=4] {'tp'}, dimensions={0} | all-to-all | bytes 4194304 | tf_op jit(solution)/shard_map/all_to_all | solution.py:53
  87.1 3.3 %reshape.82 = bf16[4096,1,256]{2,1,0:T(2,128)(2,1)} reshape(bf16[4,2,131072]{2,1,0:T(2,128)(2,1)S(1)} %all_to_all.31) | data formatting | bytes 4194304
  90.4 2.6 copy.66
  93.0 0.0 copy-start.4
  93.0 0.0 copy-start.5
  93.0 2.4 copy.57
  95.4 0.0 all-gather.3.cloned.1.call-update
  95.4 0.0 copy-done.4
  95.5 0.0 copy-done.5
  95.5 0.2 select_reduce_fusion
  95.7 0.0 reduce-scatter.2.cloned.1.call-done
  95.7 0.9 convert_element_type.34
  96.6 8.4 %all_gather.15 = bf16[16,8192]{1,0:T(8,128)(2,1)S(1)} all-gather(bf16[16,2048]{1,0:T(8,128)(2,1)S(1)} %convert_element_type.34), channel_id=1, replica_groups=mesh['replica'=8,'tp'=4] {'tp'}, dimensions={1}, use_global_device_ids=true | all-gather | bytes 327680 | tf_op jit(solution)/shard_map/all_gather | solution.py:44
  105.0 0.2 fusion.3
  105.2 0.0 all-gather.5.cloned.1.call-done
  105.2 3.8 %fusion.2 = bf16[2,2,8,128]{3,2,1,0:T(8,128)(2,1)S(1)} fusion(bf16[8192,256]{1,0:T(8,128)(2,1)} %all-gather.5.cloned.1.call-done, bf16[16,8192]{1,0:T(8,128)(2,1)S(1)} %all_gather.15, f32[8192]{0:T(1024)S(1)} %convert_element_type.36, f32[16]{0:T(128)S(1)} %add_rsqrt_fusion), kind=kOutput, calls=%fused_computation.6 | convolution fusion | flops 67637248 | bytes 4497472 | tf_op jit(solution)/shard_map/dot_general | solution.py:64
  109.0 7.4 %all_gather.19 = bf16[16,2,512]{2,0,1:T(8,128)(2,1)S(1)} all-gather(bf16[16,2,128]{2,0,1:T(8,128)(2,1)S(1)} %bitcast.65), channel_id=1, replica_groups=mesh['replica'=8,'tp'=4] {'tp'}, dimensions={2}, use_global_device_ids=true | all-gather | bytes 40960 | tf_op jit(solution)/shard_map/all_gather | solution.py:69
  116.5 7.0 %reshape.78 = bf16[8192,2,128]{2,1,0:T(2,128)(2,1)} reshape(bf16[8192,256]{1,0:T(8,128)(2,1)} %all-gather.5.cloned.1.call-done) | data formatting | bytes 8388608 | tf_op jit(solution)/shard_map/reshape | solution.py:101
  123.5 122.8 %all-gather.3.cloned.1.call-done = bf16[8192,1024]{1,0:T(8,128)(2,1)} async-done(((bf16[1024,1024]{1,0:T(8,128)(2,1)}), bf16[8192,1024]{1,0:T(8,128)(2,1)}) %all-gather.3.cloned.1.call-update) | async-done | bytes 16777232 | tf_op jit(solution)/shard_map/all_gather | solution.py:60
  246.3 0.0 copy-start.1
  246.3 0.0 slice-start
  246.3 0.0 slice-start.1
  246.3 0.0 slice-start.2
  246.3 8.2 %convolution_convert_fusion = bf16[16,1024]{1,0:T(8,128)(2,1)S(1)} fusion(bf16[8192,1024]{1,0:T(8,128)(2,1)} %all-gather.3.cloned.1.call-done, bf16[16,8192]{1,0:T(8,128)(2,1)S(1)} %all_gather.15, f32[8192]{0:T(1024)S(1)} %convert_element_type.36, f32[16]{0:T(128)S(1)} %add_rsqrt_fusion), kind=kOutput, calls=%fused_computation.4 | convolution fusion | flops 268976128 | bytes 17104960 | tf_op jit(solution)/shard_map/dot_general | solution.py:63
  254.5 0.0 copy-start
  254.5 8.7 %all_gather.17 = bf16[16,4096]{1,0:T(8,128)(2,1)S(1)} all-gather(bf16[16,1024]{1,0:T(8,128)(2,1)S(1)} %convolution_convert_fusion), channel_id=1, replica_groups=mesh['replica'=8,'tp'=4] {'tp'}, dimensions={1}, use_global_device_ids=true | all-gather | bytes 163840 | tf_op jit(solution)/shard_map/all_gather | solution.py:68
  263.3 0.1 fusion.13
  263.4 0.0 copy-done.1
  263.4 0.0 slice-start.3
  263.4 1.3 fusion.23
  264.7 0.2 fusion.7
  264.9 0.0 copy-done
  265.0 0.7 fusion.1
  265.7 0.6 copy.77
  266.3 0.0 slice-done
  266.3 0.0 slice-done.1
  266.3 0.0 slice-done.2
  266.3 0.0 slice-done.3
  266.3 6.2 %copy.80 = bf16[8192,1024]{1,0:T(8,128)(2,1)} copy(bf16[8192,1024]{1,0:T(8,128)(2,1)S(1)} %bitcast.47) | data formatting | bytes 33554432
  (16 shorter events, 0.1 us)
Async XLA Ops:
  7.2 4.8 %copy-start.3 = (bf16[256,2,512]{2,1,0:T(2,128)(2,1)S(1)}, bf16[256,2,512]{2,1,0:T(2,128)(2,1)}, u32[]{:S(2)}) copy-start(bf16[256,2,512]{2,1,0:T(2,128)(2,1)} %param.12) | copy-start | bytes 1572868
  7.2 88.5 %reduce-scatter.2.cloned.1.call-start = ((), (), s32[]{:S(2)}) async-start(), calls=%async_computation.3 | async-start | bytes 1179648 | tf_op jit(solution)/shard_map/reduce_scatter | solution.py:38
  11.8 16.2 %copy-start.2 = (bf16[256,4096]{1,0:T(8,128)(2,1)S(1)}, bf16[256,4096]{1,0:T(8,128)(2,1)}, u32[]{:S(2)}) copy-start(bf16[256,4096]{1,0:T(8,128)(2,1)} %param.11) | copy-start | bytes 6291460
  11.9 93.3 %all-gather.5.cloned.1.call-start = ((), (), s32[]{:S(2)}) async-start(), calls=%async_computation.5 | async-start | bytes 4718592 | tf_op jit(solution)/shard_map/all_gather | solution.py:61
  28.0 218.3 %all-gather.3.cloned.1.call-start = ((), (), s32[]{:S(2)}) async-start(), calls=%async_computation.4 | async-start | bytes 18874368 | tf_op jit(solution)/shard_map/all_gather | solution.py:60
  93.0 2.4 copy-start.4
  93.0 2.5 copy-start.5
  246.3 17.1 %copy-start.1 = (bf16[16,1024,128]{2,1,0:T(8,128)(2,1)S(1)}, bf16[16,1024,128]{2,1,0:T(8,128)(2,1)}, u32[]{:S(2)}) copy-start(bf16[16,1024,128]{2,1,0:T(8,128)(2,1)} %param.13) | copy-start | bytes 12582916
  246.3 20.0 %slice-start = ((s8[16777216]{0:T(1024)(128)(4,1)}), s8[4194304]{0:T(1024)(128)(4,1)S(1)}, s32[]{:S(2)}) async-start(s8[16777216]{0:T(1024)(128)(4,1)} %bitcast.46), calls=%async_computation.6 | async-start | bytes 8388608
  246.3 20.0 %slice-start.1 = ((s8[16777216]{0:T(1024)(128)(4,1)}), s8[4194304]{0:T(1024)(128)(4,1)S(1)}, s32[]{:S(2)}) async-start(s8[16777216]{0:T(1024)(128)(4,1)} %bitcast.46), calls=%async_computation.7 | async-start | bytes 8388608
  246.3 20.0 %slice-start.2 = ((s8[16777216]{0:T(1024)(128)(4,1)}), s8[4194304]{0:T(1024)(128)(4,1)S(1)}, s32[]{:S(2)}) async-start(s8[16777216]{0:T(1024)(128)(4,1)} %bitcast.46), calls=%async_computation.8 | async-start | bytes 8388608
  254.5 10.4 %copy-start = (bf16[16,1024,128]{2,1,0:T(8,128)(2,1)S(1)}, bf16[16,1024,128]{2,1,0:T(8,128)(2,1)}, u32[]{:S(2)}) copy-start(bf16[16,1024,128]{2,1,0:T(8,128)(2,1)} %param.14) | copy-start | bytes 12582916
  263.4 2.9 %slice-start.3 = ((s8[16777216]{0:T(1024)(128)(4,1)}), s8[4194304]{0:T(1024)(128)(4,1)S(1)}, s32[]{:S(2)}) async-start(s8[16777216]{0:T(1024)(128)(4,1)} %bitcast.46), calls=%async_computation.9 | async-start | bytes 8388608
Sparse Core Ops, SparseCore 0:
  12.0 35.2 reduce-scatter.1
  48.9 45.1 all-gather.4
  96.4 149.8 all-gather.2
where the time goes:
time: 280 us; the launch traced here: 279 us
  waiting for transfers between devices  123 us (44%)
  blocking collectives  65.9 us (24%)
  local copies, waits for them, and re-layouts  34.3 us (12%)
  other arithmetic  23.9 us (9%)
  matrix products  18 us (6%)
  between operations  14 us (5%)
    all_gather x1, waiting for transfers between devices, per_device(): lax.all_gather(flat_query, 'replica', axis=0, tiled=True)  123 us
    all_to_all x1, blocking collectives, per_device(): lax.all_to_all(query_rows, 'tp', split_axis=2, concat_axis=0, tiled=True)  27.9 us
    unnamed x2, other arithmetic  21.6 us
    unnamed x29, local copies, waits for them, and re-layouts  17.2 us
    all_to_all x1, blocking collectives, per_device(): lax.all_to_all(w_keyvalue, 'tp', split_axis=2, concat_axis=0, tiled=True)  13.5 us
    all_gather x1, blocking collectives, per_device(): lax.all_gather(query_local, 'tp', axis=1, tiled=True)  8.68 us
    all_gather x1, blocking collectives, per_device(): whole = lax.all_gather(embedded, 'tp', axis=1, tiled=True)  8.37 us
    dot_general x1, matrix products, per_device(): query_acc = jnp.dot(normed, query_full, preferred_element_type=jnp.float32)  8.22 us
  transfers between devices with their start and end apart: 3, of which 1 were waited for; matrix products, arithmetic and copies ran while one was open for 19% of the time, Pallas kernels for 0%

commit v1 on v0

--- a/solution.py
+++ b/solution.py
@@ -57,7 +57,10 @@
     pair_cols = pair_mid.shape[2]
     flat_pair = pair_mid.reshape(pair_mid.shape[0], 2 * pair_cols)
     query_full, pair_full = (
-        lax.all_gather(flat_query, "replica", axis=0, tiled=True),
+        jnp.concatenate(
+            lax.all_to_all(jnp.stack([flat_query] * lax.axis_size("replica")), "replica", 0, 0),
+            axis=0,
+        ),
         lax.all_gather(flat_pair, "replica", axis=0, tiled=True),
     )
     query_acc = jnp.dot(normed, query_full, preferred_element_type=jnp.float32)

time: 280 us -> 547 us (1.95)
  waiting for transfers between devices: 123 us -> 396 us
  blocking collectives: 65.9 us -> 26.8 us
  local copies, waits for them, and re-layouts: 34.3 us -> 53.9 us
  starting transfers between devices: 0.12 us -> 14.6 us
    all_to_all x0 -> x3, waiting for transfers between devices: none -> 243 us  [the longest x1 220 us: per_device(): lax.all_to_all(jnp.stack([flat_query] * lax.axis_size('replica')), 'repli...]
    all_gather x1 -> x0, waiting for transfers between devices: 123 us -> none  [per_device(): lax.all_gather(flat_query, 'replica', axis=0, tiled=True)]
    all_gather x1, waiting for transfers between devices: 0.02 us -> 82.5 us  [per_device(): lax.all_gather(flat_pair, 'replica', axis=0, tiled=True)]
    reduce_scatter x1, waiting for transfers between devices: 0.01 us -> 69.7 us  [per_device(): lax.psum_scatter(jnp.dot(onehot, embed_table, preferred_element_type=jnp....]
    all_to_all x2 -> x0, blocking collectives: 41.4 us -> none  [the longest x1 27.9 us: per_device(): lax.all_to_all(query_rows, 'tp', split_axis=2, concat_axis=0, tiled=True)]
    all_to_all x0 -> x3, starting transfers between devices: none -> 14.5 us  [the longest x1 5.87 us: per_device(): lax.all_to_all(jnp.stack([flat_query] * lax.axis_size('replica')), 'repli...]
    unnamed x29 -> x21, local copies, waits for them, and re-layouts: 17.2 us -> 27.2 us
    another operation x0 -> x1, local copies, waits for them, and re-layouts: none -> 6.16 us  [per_device(): jnp.stack([flat_query] * lax.axis_size('replica'))]
  transfers between devices with their start and end apart: 3 -> 5, of which waited for: 1 -> 4; matrix products, arithmetic and copies ran while one was open for 19% -> 5% of each run, Pallas kernels for 0% -> 0%
where the time goes in v1:
time: 547 us; the launch traced here: 545 us
  waiting for transfers between devices  396 us (72%)
  local copies, waits for them, and re-layouts  53.9 us (10%)
  blocking collectives  26.8 us (5%)
  other arithmetic  23.2 us (4%)
  matrix products  17.2 us (3%)
  starting transfers between devices  14.6 us (3%)
  between operations  14.2 us (3%)
    all_to_all x1, waiting for transfers between devices, per_device(): lax.all_to_all(jnp.stack([flat_query] * lax.axis_size('replica')), 'repli...  220 us
    all_gather x1, waiting for transfers between devices, per_device(): lax.all_gather(flat_pair, 'replica', axis=0, tiled=True)  82.5 us
    reduce_scatter x1, waiting for transfers between devices, per_device(): lax.psum_scatter(jnp.dot(onehot, embed_table, preferred_element_type=jnp....  69.7 us
    unnamed x21, local copies, waits for them, and re-layouts  27.2 us
    all_to_all x1, waiting for transfers between devices, per_device(): lax.all_to_all(query_rows, 'tp', split_axis=2, concat_axis=0, tiled=True)  22.9 us
    unnamed x1, other arithmetic  21.6 us
  transfers between devices with their start and end apart: 5, of which 4 were waited for; matrix products, arithmetic and copies ran while one was open for 5% of the time, Pallas kernels for 0%

profile of v1, /device:TPU:0, one launch (start us, length us, event | category | flops | bytes accessed | tf_op | source)
XLA Modules:
  0.0 545.4 jit_solution(15128236289440982073)
XLA Ops:
  7.2 10.0 %copy.48 = bf16[256,1,4096]{0,1,2:T(2,128)(2,1)} copy(bf16[256,1,4096]{2,0,1:T(8,128)(2,1)} %bitcast.51) | data formatting | bytes 4194304 | tf_op jit(solution)/shard_map/reshape | solution.py:51
  17.1 0.5 broadcast.61
  17.6 21.6 %reduce = bf16[4096,256]{1,0:T(8,128)(2,1)S(1)} reduce(bf16[4096,1,256]{2,1,0:T(2,128)(2,1)} %bitcast.47, bf16[]{:T(256)} %broadcast.61), dimensions={1}, to_apply=%bitcast.37.reduce_sub_computation | reduce | bytes 4194306
  39.2 0.0 copy-start.2
  39.2 2.1 reshape.83
  41.3 5.2 all-to-all-start
  46.5 0.0 copy-done.2
  46.5 2.0 copy.51
  48.5 22.9 %all-to-all-done = bf16[4,2,131072]{2,1,0:T(2,128)(2,1)S(1)} async-done(((bf16[4,2,131072]{2,1,0:T(2,128)(2,1)}), bf16[4,2,131072]{2,1,0:T(2,128)(2,1)S(1)}, u32[]{:S(2)}, u32[]{:S(2)}) %all-to-all-start) | async-done | bytes 2097184 | tf_op jit(solution)/shard_map/all_to_all | solution.py:53
  71.4 3.5 all-to-all-start.2
  74.8 3.3 reshape.84
  78.1 3.9 copy.58
  82.0 3.0 copy.49
  85.0 0.0 all-to-all-done.2
  85.0 6.2 %stack.3 = bf16[8,1024,1024]{2,1,0:T(8,128)(2,1)} broadcast(bf16[1024,1024]{1,0:T(8,128)(2,1)S(1)} %bitcast.49), dimensions={1,2} | broadcast | bytes 18874368 | tf_op jit(solution)/shard_map/stack | solution.py:61
  91.2 0.0 copy-start.4
  91.2 5.9 %all-to-all-start.1 = ((bf16[8,1024,1024]{2,1,0:T(8,128)(2,1)}), bf16[8,1024,1024]{2,1,0:T(8,128)(2,1)}, u32[]{:S(2)}, u32[]{:S(2)}) async-start(bf16[8,1024,1024]{2,1,0:T(8,128)(2,1)} %stack.3), calls=%async_computation.2 | async-start | bytes 33554432 | tf_op jit(solution)/shard_map/all_to_all | solution.py:61
  97.0 0.0 reduce-scatter.2.cloned.1.call-start
  97.1 0.0 copy-done.4
  97.1 0.0 copy-start.3
  97.1 0.0 copy-start.5
  97.1 3.9 fusion.6
  101.1 0.0 reduce-scatter.2.cloned.1.call-update
  101.1 0.0 all-gather.2.cloned.1.call-start
  101.1 0.6 copy.52
  101.8 0.9 copy.68
  102.6 0.0 all-gather.2.cloned.1.call-update
  102.7 0.0 copy-done.3
  102.7 0.0 copy-done.5
  102.7 0.2 select_reduce_fusion
  102.9 69.7 %reduce-scatter.2.cloned.1.call-done = f32[16,2048]{1,0:T(8,128)} async-done(((f32[128,2048]{1,0:T(8,128)}), f32[16,2048]{1,0:T(8,128)}) %reduce-scatter.2.cloned.1.call-update) | async-done | bytes 131088 | tf_op jit(solution)/shard_map/reduce_scatter | solution.py:38
  172.6 0.9 convert_element_type.34
  173.5 9.4 %all_gather.12 = bf16[16,8192]{1,0:T(8,128)(2,1)S(1)} all-gather(bf16[16,2048]{1,0:T(8,128)(2,1)S(1)} %convert_element_type.34), channel_id=1, replica_groups=mesh['replica'=8,'tp'=4] {'tp'}, dimensions={1}, use_global_device_ids=true | all-gather | bytes 327680 | tf_op jit(solution)/shard_map/all_gather | solution.py:44
  182.9 0.2 fusion.3
  183.1 82.5 %all-gather.2.cloned.1.call-done = bf16[8192,256]{1,0:T(8,128)(2,1)} async-done(((bf16[1024,256]{1,0:T(8,128)(2,1)}), bf16[8192,256]{1,0:T(8,128)(2,1)}) %all-gather.2.cloned.1.call-update) | async-done | bytes 4194320 | tf_op jit(solution)/shard_map/all_gather | solution.py:64
  265.6 2.9 fusion.2
  268.5 8.2 %all_gather.15 = bf16[16,2,512]{2,0,1:T(8,128)(2,1)S(1)} all-gather(bf16[16,2,128]{2,0,1:T(8,128)(2,1)S(1)} %bitcast.64), channel_id=1, replica_groups=mesh['replica'=8,'tp'=4] {'tp'}, dimensions={2}, use_global_device_ids=true | all-gather | bytes 40960 | tf_op jit(solution)/shard_map/all_gather | solution.py:72
  276.8 6.9 %reshape.80 = bf16[8192,2,128]{2,1,0:T(2,128)(2,1)} reshape(bf16[8192,256]{1,0:T(8,128)(2,1)} %all-gather.2.cloned.1.call-done) | data formatting | bytes 8388608 | tf_op jit(solution)/shard_map/reshape | solution.py:104
  283.7 220.5 %all-to-all-done.1 = bf16[8,1024,1024]{2,1,0:T(8,128)(2,1)} async-done(((bf16[8,1024,1024]{2,1,0:T(8,128)(2,1)}), bf16[8,1024,1024]{2,1,0:T(8,128)(2,1)}, u32[]{:S(2)}, u32[]{:S(2)}) %all-to-all-start.1) | async-done | bytes 16777248 | tf_op jit(solution)/shard_map/all_to_all | solution.py:61
  504.2 0.0 copy-start.1
  504.2 8.2 %convolution_convert_fusion = bf16[16,1024]{1,0:T(8,128)(2,1)S(1)} fusion(bf16[8192,1024]{1,0:T(8,128)(2,1)} %bitcast.3, bf16[16,8192]{1,0:T(8,128)(2,1)S(1)} %all_gather.12, f32[8192]{0:T(1024)S(1)} %convert_element_type.36, f32[16]{0:T(128)S(1)} %add_rsqrt_fusion), kind=kOutput, calls=%fused_computation.4 | convolution fusion | flops 268976128 | bytes 17104960 | tf_op jit(solution)/shard_map/dot_general | solution.py:66
  512.4 0.0 copy-start
  512.4 9.2 %all_gather.13 = bf16[16,4096]{1,0:T(8,128)(2,1)S(1)} all-gather(bf16[16,1024]{1,0:T(8,128)(2,1)S(1)} %convolution_convert_fusion), channel_id=1, replica_groups=mesh['replica'=8,'tp'=4] {'tp'}, dimensions={1}, use_global_device_ids=true | all-gather | bytes 163840 | tf_op jit(solution)/shard_map/all_gather | solution.py:71
  521.7 0.1 fusion.13
  521.8 0.0 copy-done.1
  521.8 1.3 fusion.23
  523.1 0.2 fusion.7
  523.3 0.0 copy-done
  523.4 0.7 fusion.1
  524.1 0.6 copy.69
  524.7 13.9 %copy.72 = bf16[8192,1024]{1,0:T(8,128)(2,1)} copy(bf16[8192,1024]{1,0:T(8,128)(2,1)} %bitcast.3) | data formatting | bytes 33554432
  (16 shorter events, 0.1 us)
Async XLA Ops:
  39.2 7.3 %copy-start.2 = (bf16[256,2,512]{2,1,0:T(2,128)(2,1)S(1)}, bf16[256,2,512]{2,1,0:T(2,128)(2,1)}, u32[]{:S(2)}) copy-start(bf16[256,2,512]{2,1,0:T(2,128)(2,1)} %param.12) | copy-start | bytes 1572868
  41.3 30.1 %all-to-all-start = ((bf16[4,2,131072]{2,1,0:T(2,128)(2,1)}), bf16[4,2,131072]{2,1,0:T(2,128)(2,1)S(1)}, u32[]{:S(2)}, u32[]{:S(2)}) async-start(bf16[4,2,131072]{2,1,0:T(2,128)(2,1)} %reshape.83), calls=%async_computation.1 | async-start | bytes 4194304 | tf_op jit(solution)/shard_map/all_to_all | solution.py:53
  71.4 13.6 %all-to-all-start.2 = ((bf16[256,2,512]{0,1,2:T(2,128)(2,1)}), bf16[256,2,512]{0,1,2:T(2,128)(2,1)S(1)}, u32[]{:S(2)}, u32[]{:S(2)}) async-start(bf16[256,2,512]{0,1,2:T(2,128)(2,1)} %copy.51), calls=%async_computation.3 | async-start | bytes 1048576 | tf_op jit(solution)/shard_map/all_to_all | solution.py:54
  91.2 5.9 %copy-start.4 = (s32[128]{0:T(128)S(1)}, s32[128]{0:T(128)}, u32[]{:S(2)}) copy-start(s32[128]{0:T(128)} %param.8) | copy-start | bytes 1540
  91.2 413.0 %all-to-all-start.1 = ((bf16[8,1024,1024]{2,1,0:T(8,128)(2,1)}), bf16[8,1024,1024]{2,1,0:T(8,128)(2,1)}, u32[]{:S(2)}, u32[]{:S(2)}) async-start(bf16[8,1024,1024]{2,1,0:T(8,128)(2,1)} %stack.3), calls=%async_computation.2 | async-start | bytes 33554432 | tf_op jit(solution)/shard_map/all_to_all | solution.py:61
  97.0 75.5 %reduce-scatter.2.cloned.1.call-start = ((), (), s32[]{:S(2)}) async-start(), calls=%async_computation.4 | async-start | bytes 1179648 | tf_op jit(solution)/shard_map/reduce_scatter | solution.py:38
  97.1 5.6 %copy-start.3 = (bf16[8192]{0:T(1024)(128)(2,1)S(1)}, bf16[8192]{0:T(1024)(128)(2,1)}, u32[]{:S(2)}) copy-start(bf16[8192]{0:T(1024)(128)(2,1)} %param.10) | copy-start | bytes 49156
  97.1 5.6 %copy-start.5 = (s32[16]{0:T(128)S(1)}, s32[16]{0:T(128)}, u32[]{:S(2)}) copy-start(s32[16]{0:T(128)} %param.15) | copy-start | bytes 196
  101.1 164.5 %all-gather.2.cloned.1.call-start = ((), (), s32[]{:S(2)}) async-start(), calls=%async_computation.5 | async-start | bytes 4718592 | tf_op jit(solution)/shard_map/all_gather | solution.py:64
  504.2 17.6 %copy-start.1 = (bf16[16,1024,128]{2,1,0:T(8,128)(2,1)S(1)}, bf16[16,1024,128]{2,1,0:T(8,128)(2,1)}, u32[]{:S(2)}) copy-start(bf16[16,1024,128]{2,1,0:T(8,128)(2,1)} %param.13) | copy-start | bytes 12582916
  512.4 10.9 %copy-start = (bf16[16,1024,128]{2,1,0:T(8,128)(2,1)S(1)}, bf16[16,1024,128]{2,1,0:T(8,128)(2,1)}, u32[]{:S(2)}) copy-start(bf16[16,1024,128]{2,1,0:T(8,128)(2,1)} %param.14) | copy-start | bytes 12582916
Sparse Core Ops, SparseCore 0:
  101.2 71.3 reduce-scatter.1
  174.2 91.3 all-gather.1
